TPU v7x, 32 devices: a whole 2x2x4 slice. The times are simulated.
32 devices in a mesh: snp: 8 (over z, y), probe: 4 (over x, core).
Axes of the slice: x: 2, y: 2, z: 4, core: 2. Of those that a mesh axis runs over, the one named last changes fastest.
Arguments:
- dosage: bfloat16 [256, 16384], P(None, 'snp'), may hold values from 0 to 2, as said below
- allele_freq: float32 [16384], P('snp'), may hold values from 0.05 to 0.5
- probes: bfloat16 [32, 256], P('probe'), may hold values from -1 to 1, as said below
Outputs:
- kin_twice: float32 [32, 256], P('probe', 'snp')
- forms: float32 [2, 32], P(None, 'probe')
- estimates: float32 [2], replicated
Inputs may be any that keep to these rules, and one draw needn't show every extreme that they name: `dosage`: whole dosages. `probes`: every entry is -1 or 1.
All inputs are finite; a program needn't handle non-finite values.
Results may differ from a plain program's by a relative error of at most 0.0032.
Values may be sent and summed in bfloat16 or wider, within the bound.
No kernel may reach another device: no remote copies, remote signals or barrier semaphores. Data moves between devices by JAX's collectives and lax.ppermute only.
A program may use at most 64 MiB of HBM per device.

v0:
```python
import jax
import jax.numpy as jnp
from jax import lax
from jax.sharding import PartitionSpec as P


def apply_columns(vectors, standard):
    projected = jnp.dot(vectors, standard, preferred_element_type=jnp.float32).astype(jnp.bfloat16)
    return lax.dot_general(
        projected, standard, (((1,), (1,)), ((), ())), preferred_element_type=jnp.float32
    )


def body(dosage, allele_freq, probes):
    snp_count = lax.axis_size("snp")
    columns = dosage.shape[1] * snp_count
    owned = dosage.shape[0] // snp_count
    samples_all = dosage.shape[0]
    probes_all = probes.shape[0] * lax.axis_size("probe")
    scaling = lax.rsqrt(2.0 * allele_freq * (1.0 - allele_freq))
    standard = ((dosage.astype(jnp.float32) - 2.0 * allele_freq) * scaling).astype(jnp.bfloat16)
    start = lax.axis_index("snp") * owned
    signs_owned = lax.dynamic_slice_in_dim(probes, start, owned, 1).astype(jnp.float32)
    partial_once = apply_columns(probes, standard)
    summed = lax.psum(partial_once, "snp") / columns
    kin_owned = lax.dynamic_slice_in_dim(summed, start, owned, 1)
    kin_round = summed.astype(jnp.bfloat16)
    local_first = jnp.sum(signs_owned * kin_owned, axis=1) / samples_all
    form_first = lax.psum(local_first, "snp")
    partial_twice = apply_columns(kin_round, standard)
    kin_twice = lax.psum_scatter(partial_twice, "snp", scatter_dimension=1, tiled=True) / columns
    local_second = jnp.sum(signs_owned * kin_twice, axis=1) / samples_all
    form_second = lax.psum(local_second, "snp")
    forms = jnp.stack([form_first, form_second])
    estimates = lax.psum(jnp.sum(forms, axis=1), "probe") / probes_all
    return (kin_twice, forms, estimates)


def solution(mesh):
    placed = (P(None, "snp"), P("snp"), P("probe", None))
    return jax.shard_map(
        body,
        mesh=mesh,
        in_specs=placed,
        out_specs=(P("probe", "snp"), P(None, "probe"), P()),
        check_vma=False,
    )
```

profile of v0, /device:TPU:0, one launch (start us, length us, event | category | flops | bytes accessed | tf_op | source)
XLA Modules:
  0.0 129.7 jit_solution(3306518735828132539)
XLA Ops:
  7.2 0.0 reduce-scatter.4.cloned.1.call-start
  7.2 0.7 broadcast_multiply_fusion.1
  7.9 0.0 copy-start.1
  7.9 2.6 %fusion = f32[8,256]{1,0:T(8,128)S(1)} fusion(bf16[8,256]{1,0:T(8,128)(2,1)} %param.5, bf16[256,2048]{1,0:T(8,128)(2,1)} %param.3, f32[2048]{0:T(1024)S(1)} %get-tuple-element.11, f32[2048]{0:T(1024)S(1)} %get-tuple-element.10), kind=kOutput, calls=%fused_computation.3 | convolution fusion | flops 20987904 | bytes 1077248 | tf_op jit(solution)/shard_map/dot_general | solution.py:9
  10.5 23.4 %psum.28 = f32[8,256]{1,0:T(8,128)S(1)} all-reduce(f32[8,256]{1,0:T(8,128)S(1)} %fusion), channel_id=1, replica_groups=mesh['snp'=8,'probe'=4] {'snp'}, use_global_device_ids=true, to_apply=%region_0.0 | all-reduce | flops 2048 | bytes 16384 | tf_op jit(solution)/shard_map/psum | solution.py:25
  34.0 0.0 copy-done.1
  34.0 0.0 copy-start
  34.0 1.3 %convolution_bitcast_fusion = f32[256,8]{1,0:T(8,128)} fusion(bf16[256,2048]{1,0:T(8,128)(2,1)S(1)} %copy-done.1, f32[2048]{0:T(1024)S(1)} %get-tuple-element.11, f32[2048]{0:T(1024)S(1)} %get-tuple-element.10, f32[8,256]{1,0:T(8,128)S(1)} %psum.28), kind=kOutput, calls=%fused_computation.4 | convolution fusion | flops 20992000 | bytes 1081344
  35.3 0.0 reduce-scatter.4.cloned.1.call-update
  35.3 59.6 %reduce-scatter.4.cloned.1.call-done = f32[32,8]{1,0:T(8,128)} async-done(((f32[256,8]{1,0:T(8,128)}), f32[32,8]{1,0:T(8,128)}) %reduce-scatter.4.cloned.1.call-update) | async-done | bytes 1040
  95.0 0.8 copy.7
  95.7 0.0 copy-done
  95.7 0.7 fusion.1
  96.5 19.5 %all-reduce = (f32[1,8]{1,0:T(1,128)S(1)}, f32[1,8]{1,0:T(1,128)S(1)}) all-reduce(f32[1,8]{1,0:T(1,128)S(1)} %get-tuple-element.12, f32[1,8]{1,0:T(1,128)S(1)} %get-tuple-element.13), channel_id=1, replica_groups=mesh['snp'=8,'probe'=4] {'snp'}, use_global_device_ids=true, to_apply=%region_5.0 | all-reduce | flops 16 | bytes 128 | tf_op jit(solution)/shard_map/psum | solution.py:33
  116.0 0.7 fusion.5
  116.7 5.7 %psum.31 = f32[2]{0:T(128)S(1)} all-reduce(f32[2]{0:T(128)S(1)} %get-tuple-element.7), channel_id=1, replica_groups=mesh['snp'=8,'probe'=4] {'probe'}, use_global_device_ids=true, to_apply=%region_7.0 | all-reduce | flops 2 | bytes 16 | tf_op jit(solution)/shard_map/psum | solution.py:35
  122.4 0.5 broadcast_multiply_fusion.3
  (2 shorter events, 0.0 us)
Async XLA Ops:
  7.2 87.8 %reduce-scatter.4.cloned.1.call-start = ((), (), s32[]{:S(2)}) async-start(), calls=%async_computation.1 | async-start | bytes 147456
  7.9 26.0 %copy-start.1 = (bf16[256,2048]{1,0:T(8,128)(2,1)S(1)}, bf16[256,2048]{1,0:T(8,128)(2,1)}, u32[]{:S(2)}) copy-start(bf16[256,2048]{1,0:T(8,128)(2,1)} %param.3) | copy-start | bytes 3145732
  34.0 61.8 %copy-start = (bf16[8,256]{1,0:T(8,128)(2,1)S(1)}, bf16[8,256]{1,0:T(8,128)(2,1)}, u32[]{:S(2)}) copy-start(bf16[8,256]{1,0:T(8,128)(2,1)} %param.5) | copy-start | bytes 12292
Sparse Core Ops, SparseCore 0:
  35.4 59.4 reduce-scatter.3
where the time goes:
time: 130 us
  waiting for transfers between devices  59.6 us (46%)
  blocking collectives  48.6 us (37%)
  between operations  14.1 us (11%)
  matrix products  3.96 us (3%)
  other arithmetic  2.65 us (2%)
    unnamed x2, waiting for transfers between devices  59.6 us
    psum x1, blocking collectives, body(): summed = lax.psum(partial_once, 'snp') / columns  23.4 us
    psum x1, blocking collectives, body(): form_second = lax.psum(local_second, 'snp')  19.5 us
    psum x1, blocking collectives, body(): estimates = lax.psum(jnp.sum(forms, axis=1), 'probe') / probes_all  5.66 us
    dot_general x1, matrix products, apply_columns(): lax.dot_general(projected, standard, (((1,), (1,)), ((), ())), preferred_...  2.63 us
  transfers between devices with their start and end apart: 1, of which 1 were waited for; matrix products, arithmetic and copies ran while one was open for 0% of the time, Pallas kernels for 0%

commit v1 on v0

--- a/solution.py
+++ b/solution.py
@@ -30,7 +30,11 @@
     partial_twice = apply_columns(kin_round, standard)
     kin_twice = lax.psum_scatter(partial_twice, "snp", scatter_dimension=1, tiled=True) / columns
     local_second = jnp.sum(signs_owned * kin_twice, axis=1) / samples_all
-    form_second = lax.psum(local_second, "snp")
+    form_second = local_second
+    for hop in (1, 2, 4):
+        form_second = form_second + lax.ppermute(
+            form_second, "snp", [(dev, dev ^ hop) for dev in range(8)]
+        )
     forms = jnp.stack([form_first, form_second])
     estimates = lax.psum(jnp.sum(forms, axis=1), "probe") / probes_all
     return (kin_twice, forms, estimates)

time: 130 us -> 140 us (1.077)
  waiting for transfers between devices: 59.6 us -> 67.7 us
  starting transfers between devices: 0.04 us -> 1.59 us
    ppermute x0 -> x3, waiting for transfers between devices: none -> 8.02 us  [body(): lax.ppermute(form_second, 'snp', [(dev, dev ^ hop) for dev in range(8)])]
    ppermute x0 -> x3, starting transfers between devices: none -> 1.56 us  [body(): lax.ppermute(form_second, 'snp', [(dev, dev ^ hop) for dev in range(8)])]
  transfers between devices with their start and end apart: 1 -> 4, of which waited for: 1 -> 3; matrix products, arithmetic and copies ran while one was open for 0% -> 0% of each run, Pallas kernels for 0% -> 0%
where the time goes in v1:
time: 140 us; the launch traced here: 139 us
  waiting for transfers between devices  67.7 us (48%)
  blocking collectives  48.6 us (35%)
  between operations  14.1 us (10%)
  matrix products  3.96 us (3%)
  other arithmetic  2.66 us (2%)
  starting transfers between devices  1.59 us (1%)
    unnamed x2, waiting for transfers between devices  59.6 us
    psum x1, blocking collectives, body(): summed = lax.psum(partial_once, 'snp') / columns  23.4 us
    psum x1, blocking collectives, body(): form_first = lax.psum(local_first, 'snp')  19.5 us
    ppermute x3, waiting for transfers between devices, body(): lax.ppermute(form_second, 'snp', [(dev, dev ^ hop) for dev in range(8)])  8.02 us
    psum x1, blocking collectives, body(): estimates = lax.psum(jnp.sum(forms, axis=1), 'probe') / probes_all  5.66 us
  transfers between devices with their start and end apart: 4, of which 3 were waited for; matrix products, arithmetic and copies ran while one was open for 0% of the time, Pallas kernels for 0%

profile of v1, /device:TPU:0, one launch (start us, length us, event | category | flops | bytes accessed | tf_op | source)
XLA Modules:
  0.0 139.3 jit_solution(8378845515362474365)
XLA Ops:
  7.2 0.0 reduce-scatter.4.cloned.1.call-start
  7.2 0.7 broadcast_multiply_fusion.1
  7.9 0.0 copy-start.1
  7.9 2.6 %fusion = f32[8,256]{1,0:T(8,128)S(1)} fusion(bf16[8,256]{1,0:T(8,128)(2,1)} %param.5, bf16[256,2048]{1,0:T(8,128)(2,1)} %param.3, f32[2048]{0:T(1024)S(1)} %get-tuple-element.9, f32[2048]{0:T(1024)S(1)} %get-tuple-element.8), kind=kOutput, calls=%fused_computation.3 | convolution fusion | flops 20987904 | bytes 1077248 | tf_op jit(solution)/shard_map/dot_general | solution.py:9
  10.5 23.4 %psum.21 = f32[8,256]{1,0:T(8,128)S(1)} all-reduce(f32[8,256]{1,0:T(8,128)S(1)} %fusion), channel_id=1, replica_groups=mesh['snp'=8,'probe'=4] {'snp'}, use_global_device_ids=true, to_apply=%region_0.0 | all-reduce | flops 2048 | bytes 16384 | tf_op jit(solution)/shard_map/psum | solution.py:25
  34.0 0.0 copy-done.1
  34.0 0.0 copy-start
  34.0 1.3 convolution_bitcast_fusion
  35.3 0.0 reduce-scatter.4.cloned.1.call-update
  35.3 59.6 %reduce-scatter.4.cloned.1.call-done = f32[32,8]{1,0:T(8,128)} async-done(((f32[256,8]{1,0:T(8,128)}), f32[32,8]{1,0:T(8,128)}) %reduce-scatter.4.cloned.1.call-update) | async-done | bytes 1040
  95.0 0.8 copy.7
  95.7 0.0 copy-done
  95.7 0.7 fusion.1
  96.5 1.5 %collective-permute-start = (f32[8]{0:T(128)S(1)}, f32[8]{0:T(128)S(1)}, u32[]{:S(2)}, u32[]{:S(2)}) collective-permute-start(f32[8]{0:T(128)S(1)} %broadcast_multiply_fusion.4), channel_id=1, source_target_pairs={{0,4},{4,0},{8,12},{12,8},{16,20},{20,16},{24,28},{28,24},{1,5},{5... | collective-permute-start | bytes 104 | tf_op jit(solution)/shard_map/ppermute | solution.py:35
  98.0 19.5 %psum.22 = f32[1,8]{1,0:T(1,128)S(1)} all-reduce(f32[1,8]{1,0:T(1,128)S(1)} %multiply_bitcast_fusion), channel_id=1, replica_groups=mesh['snp'=8,'probe'=4] {'snp'}, use_global_device_ids=true, to_apply=%region_3.0 | all-reduce | flops 8 | bytes 64 | tf_op jit(solution)/shard_map/psum | solution.py:29
  117.5 0.0 collective-permute-done
  117.5 0.1 collective-permute-start.1
  117.6 3.6 %collective-permute-done.1 = f32[8]{0:T(128)S(1)} collective-permute-done((f32[8]{0:T(128)S(1)}, f32[8]{0:T(128)S(1)}, u32[]{:S(2)}, u32[]{:S(2)}) %collective-permute-start.1) | collective-permute-done | bytes 64 | tf_op jit(solution)/shard_map/ppermute | solution.py:35
  121.2 0.0 collective-permute-start.2
  121.2 4.5 %collective-permute-done.2 = f32[8]{0:T(128)S(1)} collective-permute-done((f32[8]{0:T(128)S(1)}, f32[8]{0:T(128)S(1)}, u32[]{:S(2)}, u32[]{:S(2)}) %collective-permute-start.2) | collective-permute-done | bytes 64 | tf_op jit(solution)/shard_map/ppermute | solution.py:35
  125.6 0.7 fusion.6
  126.3 5.7 %psum.23 = f32[2]{0:T(128)S(1)} all-reduce(f32[2]{0:T(128)S(1)} %get-tuple-element.5), channel_id=1, replica_groups=mesh['snp'=8,'probe'=4] {'probe'}, use_global_device_ids=true, to_apply=%region_6.0 | all-reduce | flops 2 | bytes 16 | tf_op jit(solution)/shard_map/psum | solution.py:39
  132.0 0.5 broadcast_multiply_fusion.3
  (6 shorter events, 0.0 us)
Async XLA Ops:
  7.2 87.8 %reduce-scatter.4.cloned.1.call-start = ((), (), s32[]{:S(2)}) async-start(), calls=%async_computation.1 | async-start | bytes 147456
  7.9 26.0 %copy-start.1 = (bf16[256,2048]{1,0:T(8,128)(2,1)S(1)}, bf16[256,2048]{1,0:T(8,128)(2,1)}, u32[]{:S(2)}) copy-start(bf16[256,2048]{1,0:T(8,128)(2,1)} %param.3) | copy-start | bytes 3145732
  34.0 61.8 %copy-start = (bf16[8,256]{1,0:T(8,128)(2,1)S(1)}, bf16[8,256]{1,0:T(8,128)(2,1)}, u32[]{:S(2)}) copy-start(bf16[8,256]{1,0:T(8,128)(2,1)} %param.5) | copy-start | bytes 12292
  96.5 21.0 %collective-permute-start = (f32[8]{0:T(128)S(1)}, f32[8]{0:T(128)S(1)}, u32[]{:S(2)}, u32[]{:S(2)}) collective-permute-start(f32[8]{0:T(128)S(1)} %broadcast_multiply_fusion.4), channel_id=1, source_target_pairs={{0,4},{4,0},{8,12},{12,8},{16,20},{20,16},{24,28},{28,24},{1,5},{5... | collective-permute-start | bytes 104 | tf_op jit(solution)/shard_map/ppermute | solution.py:35
  117.5 3.6 %collective-permute-start.1 = (f32[8]{0:T(128)S(1)}, f32[8]{0:T(128)S(1)}, u32[]{:S(2)}, u32[]{:S(2)}) collective-permute-start(f32[8]{0:T(128)S(1)} %fusion.5), channel_id=1, source_target_pairs={{0,8},{4,12},{8,0},{12,4},{16,24},{20,28},{24,16},{28,20},{1,9},{5... | collective-permute-start | bytes 104 | tf_op jit(solution)/shard_map/ppermute | solution.py:35
  121.2 4.5 %collective-permute-start.2 = (f32[8]{0:T(128)S(1)}, f32[8]{0:T(128)S(1)}, u32[]{:S(2)}, u32[]{:S(2)}) collective-permute-start(f32[8]{0:T(128)S(1)} %add.23), channel_id=1, source_target_pairs={{0,16},{4,20},{8,24},{12,28},{16,0},{20,4},{24,8},{28,12},{1,17},{... | collective-permute-start | bytes 104 | tf_op jit(solution)/shard_map/ppermute | solution.py:35
Sparse Core Ops, SparseCore 0:
  35.4 59.4 reduce-scatter.3
